TPU v7x, 32 devices: a whole 2x2x4 slice. The times are simulated.
32 devices in a mesh: dp: 2 (over y), seq: 4 (over z), chan: 4 (over x, core).
Axes of the slice: x: 2, y: 2, z: 4, core: 2. Of those that a mesh axis runs over, the one named last changes fastest.
Arguments:
- layer_input: bfloat16 [2, 512, 2560], P('dp', ('seq', 'chan')), may hold values from -6 to 6
- inner_weight: bfloat16 [2560, 2560], P(None, 'chan'), may hold values from -0.125 to 0.125
- mixer_weight: bfloat16 [2560, 256], replicated, may hold values from -0.01171875 to 0.01171875
- step_weight: bfloat16 [2560, 40], P(None, 'chan'), may hold values from -0.125 to 0.125
- conv_inner: float32 [4, 2560], P(None, 'chan'), may hold values from -3 to 3
- conv_mixer: float32 [4, 256], replicated, may hold values from -3 to 3
- step_bias: float32 [40], P('chan'), may hold values from -2 to 1
- decay_log: float32 [40], P('chan'), as said below
- skip_gain: float32 [40], P('chan'), may hold values from 0.5 to 1.5
- output_grad: bfloat16 [2, 512, 2560], P('dp', 'seq', 'chan'), may hold values from -6 to 6
Outputs:
- input_grad: bfloat16 [2, 512, 2560], P('dp', ('seq', 'chan'))
- inner_weight_grad: float32 [2560, 2560], P(('dp', 'seq'), 'chan')
- mixer_weight_grad: float32 [2560, 256], P(('dp', 'seq', 'chan'))
- step_weight_grad: float32 [2560, 40], P(('dp', 'seq'), 'chan')
Inputs may be any that keep to these rules, and one draw needn't show every extreme that they name: exp(decay_log) is at least 0.2 / 512.
All inputs are finite; a program needn't handle non-finite values.
Results may differ from a plain program's by a relative error of at most 0.014.
Values may be sent and summed in bfloat16 or wider, within the bound.
A program may use at most 128 MiB of HBM per device.

v0:
```python
import math

import jax
import jax.numpy as jnp
from jax import lax
from jax.sharding import PartitionSpec as P

HDIM = 64


block_tokens = 256


def from_behind(value, axis, steps):
    count = lax.axis_size(axis)
    first, last = (max(0, -steps), min(count, count - steps))
    return lax.ppermute(value, axis, [(source, source + steps) for source in range(first, last)])


def prefix(value, axis, join, neutral):
    place = lax.axis_index(axis)
    gathered = jax.tree.map(
        lambda a, kind: lax.all_gather(a.astype(kind), axis), value, (jnp.bfloat16, jnp.bfloat16)
    )
    state = jax.tree.map(lambda a, e: jnp.zeros_like(a) + jnp.asarray(e, a.dtype), value, neutral)

    def one(hop, state):
        return join(
            state,
            jax.tree.map(
                lambda a, own: lax.dynamic_index_in_dim(a, hop, 0, False).astype(own.dtype),
                gathered,
                value,
            ),
        )

    return lax.fori_loop(0, place, one, state)


def prefix_2(value, axis, combine, identity):
    size, index = (lax.axis_size(axis), lax.axis_index(axis))
    everything = jax.tree.map(lambda part: lax.all_gather(part, axis), value)
    start = jax.tree.map(
        lambda part, zero: jnp.broadcast_to(jnp.asarray(zero, part.dtype), part.shape),
        value,
        identity,
    )

    def hop(k, before):
        at = size - 1 - k
        reached = at > index
        new = combine(before, jax.tree.map(lambda part: part[at], everything))
        return jax.tree.map(lambda a, b: jnp.where(reached, a, b), new, before)

    return lax.fori_loop(0, size, hop, start)


def conv_silu(inputs, history, kernel):
    length = inputs.shape[0]
    padded = jnp.concatenate([history, inputs], axis=0)
    summed = kernel[0][None, :] * padded[0:length]
    for offset in range(1, kernel.shape[0]):
        summed = summed + kernel[offset][None, :] * padded[offset : offset + length]
    return jax.nn.silu(summed)


def activations(
    inner_proj,
    mixer_proj,
    step_raw,
    inner_hist,
    mixer_hist,
    conv_inner,
    conv_mixer,
    step_bias,
    decay_log,
):
    length = inner_proj.shape[0]
    head_count = step_bias.shape[0]
    state_width = mixer_proj.shape[1] // 2
    inner_act = conv_silu(inner_proj, inner_hist, conv_inner).reshape(length, head_count, -1)
    mixer_act = conv_silu(mixer_proj, mixer_hist, conv_mixer)
    step_size = jax.nn.softplus(step_raw + step_bias[None, :])
    log_decay = -step_size * jnp.exp(decay_log)[None, :]
    return (inner_act, mixer_act[:, :state_width], mixer_act[:, state_width:], step_size, log_decay)


def spanned_scan(inner_act, input_mix, output_mix, step_size, log_decay, skip_gain, initial):
    length, head_count, head_dim = inner_act.shape
    block_len = min(block_tokens, length)
    blocks = length // block_len
    highest = lax.Precision.HIGHEST

    def to_blocks(values):
        return values.reshape((blocks, block_len) + values.shape[1:])

    def advance(carry_state, pieces):
        part_inner, part_input, part_output, part_step, part_decay = pieces
        cumulative = jnp.cumsum(part_decay, axis=0)
        scores = jnp.dot(part_output, part_input.T, precision=highest)
        causal = (jnp.arange(block_len)[:, None] >= jnp.arange(block_len)[None, :])[:, :, None]
        spread = cumulative[:, None, :] - cumulative[None, :, :]
        weights = jnp.where(causal, jnp.exp(jnp.where(causal, spread, 0.0)), 0.0)
        weights = weights * scores[:, :, None] * part_step[None, :, :]
        within = jnp.einsum("ijh,jhp->ihp", weights, part_inner, precision=highest)
        carried = jnp.exp(cumulative)[:, :, None] * jnp.einsum(
            "in,hpn->ihp", part_output, carry_state, precision=highest
        )
        result = within + carried + skip_gain[None, :, None] * part_inner
        tail_weight = jnp.exp(cumulative[-1][None, :] - cumulative) * part_step
        update_term = jnp.einsum(
            "jh,jhp,jn->hpn", tail_weight, part_inner, part_input, precision=highest
        )
        carry_state = jnp.exp(cumulative[-1])[:, None, None] * carry_state + update_term
        return (carry_state, result)

    final, results = lax.scan(
        advance,
        initial,
        (
            to_blocks(inner_act),
            to_blocks(input_mix),
            to_blocks(output_mix),
            to_blocks(step_size),
            to_blocks(log_decay),
        ),
    )
    return (results.reshape(length, head_count, head_dim), final)


def combine_carry(earlier, latter):
    return (earlier[0] + latter[0], jnp.exp(latter[0])[:, None, None] * earlier[1] + latter[1])


def contract_rows(left_rows, right_rows):
    return lax.dot_general(
        left_rows, right_rows, (((0,), (0,)), ((), ())), preferred_element_type=jnp.float32
    )


def project_back(gradient, weight):
    return lax.dot_general(
        gradient, weight, (((1,), (1,)), ((), ())), preferred_element_type=jnp.float32
    )


def split_pair(values):
    leading = values.astype(jnp.bfloat16)
    residue = (values - leading.astype(jnp.float32)).astype(jnp.bfloat16)
    return (leading, residue)


def body(
    layer_input,
    inner_weight,
    mixer_weight,
    step_weight,
    conv_inner,
    conv_mixer,
    step_bias,
    decay_log,
    skip_gain,
    output_grad,
):
    gathered = lax.all_gather(layer_input[0], "chan", axis=0, tiled=True)
    seg_len = gathered.shape[0]
    chan_count = lax.axis_size("chan")
    history_len = conv_inner.shape[0] - 1
    highest = lax.Precision.HIGHEST
    inner_proj = jnp.dot(gathered, inner_weight, preferred_element_type=jnp.float32).astype(
        jnp.bfloat16
    )
    mixer_proj = jnp.dot(gathered, mixer_weight, preferred_element_type=jnp.float32).astype(
        jnp.bfloat16
    )
    step_raw = jnp.dot(gathered, step_weight, preferred_element_type=jnp.float32)
    inner_hist, mixer_hist = from_behind(
        (inner_proj[seg_len - history_len :], mixer_proj[seg_len - history_len :]), "seq", 1
    )
    inner_wide = lax.optimization_barrier(inner_proj).astype(jnp.float32)
    mixer_wide = lax.optimization_barrier(mixer_proj).astype(jnp.float32)
    inner_prev = lax.optimization_barrier(inner_hist).astype(jnp.float32)
    mixer_prev = lax.optimization_barrier(mixer_hist).astype(jnp.float32)

    def local_acts(inner_in, mixer_in, step_in, inner_before, mixer_before):
        return activations(
            inner_in,
            mixer_in,
            step_in,
            inner_before,
            mixer_before,
            conv_inner,
            conv_mixer,
            step_bias,
            decay_log,
        )

    acts, pull_acts = jax.vjp(local_acts, inner_wide, mixer_wide, step_raw, inner_prev, mixer_prev)
    inner_act, input_mix, output_mix, step_size, log_decay = acts
    head_count = step_bias.shape[0]
    upstream = output_grad[0].astype(jnp.float32).reshape(seg_len, head_count, HDIM)
    cumulative = jnp.cumsum(log_decay, axis=0)
    segment_decay = cumulative[-1]
    local_state = jnp.einsum(
        "th,thp,tn->hpn",
        jnp.exp(segment_decay[None, :] - cumulative) * step_size,
        inner_act,
        input_mix,
        precision=highest,
    )
    local_grad = jnp.einsum(
        "th,thp,tn->hpn", jnp.exp(cumulative), upstream, output_mix, precision=highest
    )
    neutral = (jnp.zeros_like(segment_decay), jnp.zeros_like(local_state))
    start_state = prefix((segment_decay, local_state), "seq", combine_carry, neutral)[1]
    end_grad = prefix_2((segment_decay, local_grad), "seq", combine_carry, neutral)[1]

    def scan_local(inner_in, input_in, output_in, step_in, decay_in):
        return spanned_scan(
            inner_in, input_in, output_in, step_in, decay_in, skip_gain, start_state
        )

    unused, pull_scan = jax.vjp(scan_local, inner_act, input_mix, output_mix, step_size, log_decay)
    act_grads = pull_scan((upstream, end_grad))
    inner_local, mixer_local, step_local, inner_back, mixer_back = pull_acts(act_grads)
    inner_next, mixer_next = from_behind((inner_back, mixer_back), "seq", -1)
    keep_rows = seg_len - history_len
    inner_total = jnp.concatenate(
        [inner_local[:keep_rows], inner_local[keep_rows:] + inner_next], axis=0
    )
    grad_mixer = jnp.concatenate(
        [mixer_local[:keep_rows], mixer_local[keep_rows:] + mixer_next], axis=0
    )
    grad_inner = inner_total.astype(jnp.bfloat16)
    grad_step = step_local.astype(jnp.bfloat16)
    mixer_lead, mixer_rest = split_pair(grad_mixer)
    inner_rows, step_rows, lead_rows, rest_rows = (
        lax.all_to_all(grad_inner, "chan", split_axis=0, concat_axis=1, tiled=True),
        lax.all_to_all(grad_step, "chan", split_axis=0, concat_axis=1, tiled=True),
        lax.all_to_all(mixer_lead, "chan", split_axis=0, concat_axis=1, tiled=True),
        lax.all_to_all(mixer_rest, "chan", split_axis=0, concat_axis=1, tiled=True),
    )
    inner_full, step_full = (
        lax.all_gather(inner_weight, "chan", axis=1, tiled=True),
        lax.all_gather(step_weight, "chan", axis=1, tiled=True),
    )
    row_count = seg_len // chan_count
    mixer_rows = lead_rows.astype(jnp.float32) + rest_rows.astype(jnp.float32)
    mixer_rows = jnp.sum(mixer_rows.reshape(row_count, chan_count, -1), axis=1)
    rows_lead, rows_rest = split_pair(mixer_rows)
    summed = project_back(inner_rows, inner_full) + project_back(step_rows, step_full)
    summed = summed + project_back(rows_lead, mixer_weight) + project_back(rows_rest, mixer_weight)
    input_grad = summed.astype(jnp.bfloat16)
    token_count = seg_len * lax.axis_size("seq") * lax.axis_size("dp")
    norm_factor = 1.0 / math.sqrt(token_count)
    inner_term = contract_rows(gathered, grad_inner) * norm_factor
    step_term = contract_rows(gathered, grad_step) * norm_factor
    mixer_term = (
        contract_rows(gathered, mixer_lead) + contract_rows(gathered, mixer_rest)
    ) * norm_factor
    mixer_weight_grad = lax.psum_scatter(
        mixer_term, ("dp", "seq", "chan"), scatter_dimension=0, tiled=True
    )
    inner_weight_grad, step_weight_grad = (
        lax.psum_scatter(inner_term, ("dp", "seq"), scatter_dimension=0, tiled=True),
        lax.psum_scatter(step_term, ("dp", "seq"), scatter_dimension=0, tiled=True),
    )
    return (input_grad[None], inner_weight_grad, mixer_weight_grad, step_weight_grad)


def solution(mesh):
    in_specs = (
        P("dp", ("seq", "chan"), None),
        P(None, "chan"),
        P(),
        P(None, "chan"),
        P(None, "chan"),
        P(),
        P("chan"),
        P("chan"),
        P("chan"),
        P("dp", "seq", "chan"),
    )
    out_specs = (
        P("dp", ("seq", "chan"), None),
        P(("dp", "seq"), "chan"),
        P(("dp", "seq", "chan"), None),
        P(("dp", "seq"), "chan"),
    )
    return jax.shard_map(body, mesh=mesh, in_specs=in_specs, out_specs=out_specs, check_vma=False)
```

profile of v0, /device:TPU:0, one launch (start us, length us, event | category | flops | bytes accessed | tf_op | source)
XLA Modules:
  0.0 439.2 jit_solution(13962226168457161180)
XLA Ops:
  8.1 9.7 %all-gather = bf16[1,128,2560]{2,1,0:T(8,128)(2,1)S(1)} all-gather(bf16[1,32,2560]{2,1,0:T(8,128)(2,1)} %param.14), channel_id=2, replica_groups=mesh['dp'=2,'seq'=4,'chan'=4] {'chan'}, dimensions={1}, use_global_device_ids=true | all-gather | bytes 819200 | tf_op jit(solution)/shard_map/all_gather | solution.py:165
  18.2 3.5 collective-permute-start
  27.2 3.9 collective-permute-start.1
  31.3 9.3 %all-gather.4 = bf16[4,1,10]{2,1,0:T(2,128)(2,1)S(1)} all-gather(bf16[1,1,10]{2,1,0:T(2,128)(2,1)S(1)} %bitcast.159), channel_id=1, replica_groups=mesh['dp'=2,'seq'=4,'chan'=4] {'seq'}, dimensions={0}, use_global_device_ids=true | all-gather | bytes 100 | tf_op jit(solution)/shard_map/all_gather | solution.py:23
  40.8 9.3 %all-gather.3 = f32[4,1,10]{2,1,0:T(1,128)S(1)} all-gather(f32[1,1,10]{2,1,0:T(1,128)S(1)} %bitcast.149), channel_id=1, replica_groups=mesh['dp'=2,'seq'=4,'chan'=4] {'seq'}, dimensions={0}, use_global_device_ids=true | all-gather | bytes 200 | tf_op jit(solution)/shard_map/all_gather | solution.py:42
  52.7 5.9 %all-gather.11.cloned.1.call-done = f32[40,64,128]{2,1,0:T(8,128)} async-done(((f32[10,64,128]{2,1,0:T(8,128)}), f32[40,64,128]{2,1,0:T(8,128)}) %all-gather.11.cloned.1.call-update) | async-done | bytes 1310736 | tf_op jit(solution)/shard_map/all_gather | solution.py:42
  58.7 4.5 %while.23 = (s32[]{:T(128)}, f32[10,64,128]{2,1,0:T(8,128)S(1)}, s32[]{:T(128)}, f32[4,10]{1,0:T(4,128)S(1)}, f32[4,10,64,128]{3,2,1,0:T(8,128)}, /*index=5*/s32[]{:T(128)}, s32[]{:T(128)}, s32[]{:T(128)}, s32[]{:T(128)}) while((s32[]{:T(128)}, f32[10,64,128]{2,1,0:T(8,128)S(1)}, s32[]{:T(128)}, f32[4,10]{1,0:T(4,128)S(1)}, ...), condition=%wide.region_2.3_spmd.clone, body=%wide.region_1.2_spmd.clone.sunk | while | flops 327688 | bytes 983327 | solution.py:55
  65.0 16.7 %all-gather.2 = bf16[40,64,128]{2,1,0:T(8,128)(2,1)} all-gather(bf16[10,64,128]{2,1,0:T(8,128)(2,1)S(1)} %convolution_convert_fusion), channel_id=4, replica_groups=mesh['dp'=2,'seq'=4,'chan'=4] {'seq'}, dimensions={0}, use_global_device_ids=true | all-gather | bytes 819200 | tf_op jit(solution)/shard_map/all_gather | solution.py:23
  92.9 4.1 collective-permute-done.3
  99.6 3.6 copy.76
  106.8 4.2 collective-permute-done.2
  111.7 4.7 %multiply_bitcast_fusion = f32[2560,640]{0,1:T(8,128)} fusion(bf16[128,640]{1,0:T(8,128)(2,1)} %maximum_convert_fusion, bf16[1,128,2560]{2,1,0:T(8,128)(2,1)S(1)} %all-gather), kind=kOutput, calls=%fused_computation.5 | convolution fusion | flops 421068800 | bytes 7372800 | tf_op jit(solution)/shard_map/dot_general | solution.py:136
  116.4 8.2 %copy.74 = f32[2560,640]{1,0:T(8,128)} copy(f32[2560,640]{0,1:T(8,128)} %multiply_bitcast_fusion) | data formatting | bytes 13107200
  126.1 3.2 all-to-all-start.1
  130.0 3.3 all-to-all-done.1
  133.2 7.4 %all_to_all.55 = bf16[4,32,256]{2,1,0:T(8,128)(2,1)S(1)} all-to-all(bf16[4,32,256]{2,1,0:T(8,128)(2,1)S(1)} %get-tuple-element.587), channel_id=1, replica_groups=mesh['dp'=2,'seq'=4,'chan'=4] {'chan'}, dimensions={0} | all-to-all | bytes 131072 | tf_op jit(solution)/shard_map/all_to_all | solution.py:240
  140.6 3.3 all-to-all-start.3
  143.9 9.3 %all-gather.5 = bf16[4,10,2560]{2,1,0:T(8,128)(2,1)S(1)} all-gather(bf16[1,10,2560]{2,1,0:T(8,128)(2,1)S(1)} %bitcast.147), channel_id=1, replica_groups=mesh['dp'=2,'seq'=4,'chan'=4] {'chan'}, dimensions={0}, use_global_device_ids=true | all-gather | bytes 256000 | tf_op jit(solution)/shard_map/all_gather | solution.py:245
  153.4 3.4 all-to-all-start
  156.8 7.0 %all-to-all-done = bf16[4,32,640]{2,1,0:T(8,128)(2,1)S(1)} async-done(((bf16[4,32,640]{2,1,0:T(8,128)(2,1)}), bf16[4,32,640]{2,1,0:T(8,128)(2,1)S(1)}, u32[]{:S(2)}, u32[]{:S(2)}) %all-to-all-start) | async-done | bytes 163872 | tf_op jit(solution)/shard_map/all_to_all | solution.py:238
  165.6 19.5 %all-gather.9.cloned.1.call-done = bf16[2560,2560]{1,0:T(8,128)(2,1)} async-done(((bf16[2560,640]{1,0:T(8,128)(2,1)}), bf16[2560,2560]{1,0:T(8,128)(2,1)}) %all-gather.9.cloned.1.call-update) | async-done | bytes 13107216 | tf_op jit(solution)/shard_map/all_gather | solution.py:244
  185.1 8.6 %fusion.88 = f32[32,2560]{1,0:T(8,128)S(1)} fusion(bf16[32,2560]{1,0:T(8,128)(2,1)S(1)} %bitcast.145, bf16[2560,2560]{1,0:T(8,128)(2,1)} %all-gather.9.cloned.1.call-done), kind=kOutput, calls=%fused_computation.165 | convolution fusion | flops 419430400 | bytes 13598720 | tf_op jit(solution)/shard_map/dot_general | solution.py:142
  195.7 113.7 %reduce-scatter.12.cloned.1.call-done = f32[80,256]{1,0:T(8,128)} async-done(((f32[2560,256]{1,0:T(8,128)}), f32[80,256]{1,0:T(8,128)}) %reduce-scatter.12.cloned.1.call-update) | async-done | bytes 81936
  309.4 122.7 %reduce-scatter.10.cloned.1.call-done = f32[320,640]{1,0:T(8,128)} async-done(((f32[2560,640]{1,0:T(8,128)}), f32[320,640]{1,0:T(8,128)}) %reduce-scatter.10.cloned.1.call-update) | async-done | bytes 819216
  (188 shorter events, 38.4 us)
Async XLA Ops:
  8.0 13.7 %copy-start.38 = (f32[10]{0:T(128)S(1)}, f32[10]{0:T(128)}, u32[]{:S(2)}) copy-start(f32[10]{0:T(128)} %param.21) | copy-start | bytes 124
  8.0 13.7 %copy-start.5 = (bf16[2560,10]{0,1:T(8,128)(2,1)S(1)}, bf16[2560,10]{0,1:T(8,128)(2,1)}, u32[]{:S(2)}) copy-start(bf16[2560,10]{0,1:T(8,128)(2,1)} %param.17) | copy-start | bytes 153604
  8.0 13.7 %copy-start.39 = (f32[10]{0:T(128)S(1)}, f32[10]{0:T(128)}, u32[]{:S(2)}) copy-start(f32[10]{0:T(128)} %param.20) | copy-start | bytes 124
  8.0 14.6 %copy-start.36 = (f32[4,256]{1,0:T(4,128)S(1)}, f32[4,256]{1,0:T(4,128)}, u32[]{:S(2)}) copy-start(f32[4,256]{1,0:T(4,128)} %param.19) | copy-start | bytes 12292
  8.1 15.0 %copy-start.4 = (bf16[1,128,640]{2,1,0:T(8,128)(2,1)S(1)}, bf16[1,128,640]{2,1,0:T(8,128)(2,1)}, u32[]{:S(2)}) copy-start(bf16[1,128,640]{2,1,0:T(8,128)(2,1)} %param.23) | copy-start | bytes 491524
  8.1 50.6 %all-gather.11.cloned.1.call-start = ((), (), s32[]{:S(2)}) async-start(), calls=%async_computation.8 | async-start | bytes 1638400 | tf_op jit(solution)/shard_map/all_gather | solution.py:42
  18.2 5.1 %collective-permute-start = (bf16[3,256]{1,0:T(4,128)(2,1)S(1)}, bf16[3,256]{1,0:T(4,128)(2,1)S(1)}, u32[]{:S(2)}, u32[]{:S(2)}) collective-permute-start(bf16[3,256]{1,0:T(4,128)(2,1)S(1)} %slice.103), channel_id=1, source_target_pairs={{0,4},{4,8},{8,12},{1,5},{5,9},{9,13},{2,6},{6,10},{10,14},{3,7},{... | collective-permute-start | bytes 4616 | tf_op jit(solution)/shard_map/ppermute | solution.py:17
  24.5 25.7 %copy-start.25 = (f32[4,640]{1,0:T(4,128)S(1)}, f32[4,640]{1,0:T(4,128)}, u32[]{:S(2)}) copy-start(f32[4,640]{1,0:T(4,128)} %param.18) | copy-start | bytes 30724
  24.5 139.4 %reduce-scatter.14.cloned.1.call-start = ((), (), s32[]{:S(2)}) async-start(), calls=%async_computation.11 | async-start | bytes 1474560
  27.2 23.3 %collective-permute-start.1 = (bf16[3,640]{1,0:T(4,128)(2,1)S(1)}, bf16[3,640]{1,0:T(4,128)(2,1)S(1)}, u32[]{:S(2)}, u32[]{:S(2)}) collective-permute-start(bf16[3,640]{1,0:T(4,128)(2,1)S(1)} %slice.111), channel_id=1, source_target_pairs={{0,4},{4,8},{8,12},{1,5},{5,9},{9,13},{2,6},{6,10},{10,14},{3,7},{... | collective-permute-start | bytes 11528 | tf_op jit(solution)/shard_map/ppermute | solution.py:17
  40.8 43.3 %copy-start.24 = (f32[10]{0:T(128)}, f32[10]{0:T(128)S(1)}, u32[]{:S(2)}) copy-start(f32[10]{0:T(128)S(1)} %slice_reduce_fusion) | copy-start | bytes 124
  50.2 32.4 %copy-start.22 = (pred[128,128]{1,0:T(8,128)(4,1)}, pred[128,128]{1,0:T(8,128)(4,1)S(1)}, u32[]{:S(2)}) copy-start(pred[128,128]{1,0:T(8,128)(4,1)S(1)} %iota_compare_fusion) | copy-start | bytes 49156
  50.5 32.1 %copy-start.10 = (f32[128,128]{1,0:T(8,128)}, f32[128,128]{1,0:T(8,128)S(1)}, u32[]{:S(2)}) copy-start(f32[128,128]{1,0:T(8,128)S(1)} %fusion.64) | copy-start | bytes 196612
  64.5 17.1 %copy-start.7 = (f32[128,10]{0,1:T(8,128)}, f32[128,10]{0,1:T(8,128)S(1)}, u32[]{:S(2)}) copy-start(f32[128,10]{0,1:T(8,128)S(1)} %get-tuple-element.603) | copy-start | bytes 15364
  64.6 18.0 %copy-start.34 = (f32[128,10]{0,1:T(8,128)}, f32[128,10]{0,1:T(8,128)S(1)}, u32[]{:S(2)}) copy-start(f32[128,10]{0,1:T(8,128)S(1)} %get-tuple-element.604) | copy-start | bytes 15364
  88.8 96.3 %all-gather.9.cloned.1.call-start = ((), (), s32[]{:S(2)}) async-start(), calls=%async_computation.7 | async-start | bytes 16384000 | tf_op jit(solution)/shard_map/all_gather | solution.py:244
  89.3 220.1 %reduce-scatter.12.cloned.1.call-start = ((), (), s32[]{:S(2)}) async-start(), calls=%async_computation.10 | async-start | bytes 2703360
  91.5 5.5 %collective-permute-start.3 = (f32[3,256]{1,0:T(4,128)S(1)}, f32[3,256]{1,0:T(4,128)S(1)}, u32[]{:S(2)}, u32[]{:S(2)}) collective-permute-start(f32[3,256]{1,0:T(4,128)S(1)} %pad_add_fusion.3), channel_id=1, source_target_pairs={{4,0},{8,4},{12,8},{5,1},{9,5},{13,9},{6,2},{10,6},{14,10},{7,3},{... | collective-permute-start | bytes 9224 | tf_op jit(solution)/shard_map/ppermute | solution.py:17
  103.3 328.8 %reduce-scatter.10.cloned.1.call-start = ((), (), s32[]{:S(2)}) async-start(), calls=%async_computation.9 | async-start | bytes 7372800
  105.3 5.7 %collective-permute-start.2 = (f32[3,640]{1,0:T(4,128)S(1)}, f32[3,640]{1,0:T(4,128)S(1)}, u32[]{:S(2)}, u32[]{:S(2)}) collective-permute-start(f32[3,640]{1,0:T(4,128)S(1)} %pad_add_fusion.2), channel_id=1, source_target_pairs={{4,0},{8,4},{12,8},{5,1},{9,5},{13,9},{6,2},{10,6},{14,10},{7,3},{... | collective-permute-start | bytes 23048 | tf_op jit(solution)/shard_map/ppermute | solution.py:17
  124.6 19.3 %copy-start.6 = (bf16[2560,10]{0,1:T(8,128)(2,1)S(1)}, bf16[2560,10]{0,1:T(8,128)(2,1)}, u32[]{:S(2)}) copy-start(bf16[2560,10]{0,1:T(8,128)(2,1)} %param.17) | copy-start | bytes 153604
  126.1 7.2 %all-to-all-start.1 = ((bf16[4,2,160]{2,1,0:T(2,128)(2,1)}), bf16[4,2,160]{2,1,0:T(2,128)(2,1)S(1)}, u32[]{:S(2)}, u32[]{:S(2)}) async-start(bf16[4,2,160]{2,1,0:T(2,128)(2,1)} %reshape.372), calls=%async_computation.1 | async-start | bytes 8192 | tf_op jit(solution)/shard_map/all_to_all | solution.py:239
  140.6 12.8 %all-to-all-start.3 = ((bf16[4,32,256]{2,1,0:T(8,128)(2,1)}), bf16[4,32,256]{2,1,0:T(8,128)(2,1)S(1)}, u32[]{:S(2)}, u32[]{:S(2)}) async-start(bf16[4,32,256]{2,1,0:T(8,128)(2,1)} %get-tuple-element.586), calls=%async_computation.3 | async-start | bytes 131072 | tf_op jit(solution)/shard_map/all_to_all | solution.py:241
  153.4 10.5 %all-to-all-start = ((bf16[4,32,640]{2,1,0:T(8,128)(2,1)}), bf16[4,32,640]{2,1,0:T(8,128)(2,1)S(1)}, u32[]{:S(2)}, u32[]{:S(2)}) async-start(bf16[4,32,640]{2,1,0:T(8,128)(2,1)} %bitcast.15), calls=%async_computation | async-start | bytes 327680 | tf_op jit(solution)/shard_map/all_to_all | solution.py:238
  (29 other events, 98.8 us)
Sparse Core Ops, SparseCore 0:
  24.6 33.9 all-gather.10
  88.8 68.8 reduce-scatter.13
  160.5 148.8 reduce-scatter.11
  313.4 118.5 reduce-scatter.9
Sparse Core Ops, SparseCore 1:
  90.8 94.2 all-gather.8
where the time goes:
time: 440 us; the launch traced here: 439 us
  waiting for transfers between devices  281 us (64%)
  blocking collectives  61.7 us (14%)
  matrix products  29.3 us (7%)
  local copies, waits for them, and re-layouts  20.6 us (5%)
  starting transfers between devices  20.2 us (5%)
  between operations  16 us (4%)
  other arithmetic  10 us (2%)
    unnamed x8, waiting for transfers between devices  237 us
    all_gather x2, blocking collectives, prefix(): lax.all_gather(a.astype(kind), axis)  25.9 us
    all_gather x1, waiting for transfers between devices, body(): lax.all_gather(inner_weight, 'chan', axis=1, tiled=True)  19.5 us
    unnamed x91, local copies, waits for them, and re-layouts  18.1 us
    dot_general x4, matrix products, project_back(): lax.dot_general(gradient, weight, (((1,), (1,)), ((), ())), preferred_ele...  10.6 us
    ppermute x4, starting transfers between devices, from_behind(): lax.ppermute(value, axis, [(source, source + steps) for source in range(f...  9.96 us
    all_gather x1, blocking collectives, body(): gathered = lax.all_gather(layer_input[0], 'chan', axis=0, tiled=True)  9.7 us
    all_gather x1, blocking collectives, body(): lax.all_gather(step_weight, 'chan', axis=1, tiled=True)  9.33 us
  transfers between devices with their start and end apart: 12, of which 8 were waited for; matrix products, arithmetic and copies ran while one was open for 10% of the time, Pallas kernels for 0%

commit v1 on v0

v1 whole, which is shorter than its diff:
```python
import functools
import math

import jax
import jax.numpy as jnp
from jax import lax
from jax.experimental import pallas as pl
from jax.experimental.pallas import tpu as pltpu
from jax.sharding import PartitionSpec as P

MESH = pl.DeviceIdType.MESH
HDIM = 64
PAD = 16
LANES = 128
LIMIT = 60 * 2**20
BF = jnp.bfloat16
F32 = jnp.float32
HIGH = lax.Precision.HIGHEST


def size_of(axes, sizes):
    return math.prod(sizes[a] for a in axes)


def index_of(axes, sizes):
    index = 0
    for a in axes:
        index = index * sizes[a] + lax.axis_index(a)
    return index


def coords(axes, sizes, index):
    place = {}
    for a in reversed(axes):
        place[a] = lax.rem(index, sizes[a])
        index = lax.div(index, sizes[a])
    return place


def each(n, step):
    if n <= 12:
        for d in range(1, n):
            step(d)
    else:

        def one(d, carry):
            step(d)
            return carry

        lax.fori_loop(1, n, one, 0)


def exchange_kernel(jobs, tail, plugged, sizes, *refs):
    count = len(jobs)
    extra = 1 if tail else 0
    fed = count + (1 if tail == "up" else 0)
    plug_ins, plug_outs, plug_scratch = plugged.counts if plugged else (0, 0, 0)
    cuts = (fed, plug_ins, count + extra, plug_outs, 2 * (count + extra), plug_scratch)
    groups, at = [], 0
    for cut in cuts:
        groups.append(refs[at : at + cut])
        at += cut
    ins, plug_in, outs, plug_out, sems, scratch = groups
    plug = plugged.bind(sizes, plug_in, plug_out, scratch) if plugged else None
    barrier = pltpu.get_barrier_semaphore()
    chans, seqs = sizes["chan"], sizes["seq"]
    greeted = 0
    for axes in dict.fromkeys(job[0] for job in jobs):
        n, me = size_of(axes, sizes), index_of(axes, sizes)

        def greet(d, axes=axes, n=n, me=me):
            where = coords(axes, sizes, lax.rem(me + d, n))
            pl.semaphore_signal(barrier, inc=1, device_id=where, device_id_type=MESH)

        each(n, greet)
        greeted += n - 1
    if tail:
        spot = lax.axis_index("seq")
        after, before = lax.rem(spot + 1, seqs), lax.rem(spot + seqs - 1, seqs)
        ending = lax.axis_index("chan") == chans - 1
        source = {"seq": before, "chan": jnp.int32(chans - 1)}
        signal_to(barrier, source if tail == "up" else {"seq": before})

        if tail == "up":

            @pl.when(ending)
            def _():
                for c in range(chans):
                    signal_to(barrier, {"seq": after, "chan": jnp.int32(c)})

            greeted += 1 + chans * lax.div(lax.axis_index("chan"), chans - 1)
        else:
            signal_to(barrier, {"seq": after})
            greeted += 2
    if plug:
        greeted += plug.greet(barrier)
    pl.semaphore_wait(barrier, greeted)
    if plug:
        plug.start()

    def describe(k, q, landing, signal):
        axes, mode = jobs[k]
        src = ins[k] if mode == "gather" else ins[k].at[:, q] if mode == "cross" else ins[k].at[q]
        return pltpu.make_async_remote_copy(
            src_ref=src,
            dst_ref=outs[k].at[landing],
            send_sem=sems[2 * k].at[q],
            recv_sem=sems[2 * k + 1].at[signal],
            device_id=coords(axes, sizes, q),
            device_id_type=MESH,
        )

    for k, (axes, mode) in enumerate(jobs):
        n, me = size_of(axes, sizes), index_of(axes, sizes)
        each(n, lambda d, k=k, n=n, me=me: describe(k, lax.rem(me + d, n), me, me).start())
    if tail:
        tail_out = outs[count]
        tail_in = ins[count] if tail == "up" else ins[0].at[pl.ds(ins[0].shape[0] - PAD, PAD)]
        tail_send, tail_recv = sems[2 * count], sems[2 * count + 1]

        def down(c):
            return pltpu.make_async_remote_copy(
                src_ref=tail_in if c == chans - 1 else tail_out,
                dst_ref=tail_out,
                send_sem=tail_send.at[c],
                recv_sem=tail_recv.at[0],
                device_id={"seq": after} if c == chans - 1 else {"chan": jnp.int32(c)},
                device_id_type=MESH,
            )

        def up(slot):
            return pltpu.make_async_remote_copy(
                src_ref=tail_in,
                dst_ref=tail_out.at[slot],
                send_sem=tail_send.at[0],
                recv_sem=tail_recv.at[slot],
                device_id=source,
                device_id_type=MESH,
            )

        if tail == "down":

            @pl.when(ending)
            def _():
                down(chans - 1).start()
        else:
            up(lax.axis_index("chan")).start()
    for k, (axes, mode) in enumerate(jobs):
        me = index_of(axes, sizes)
        kept = ins[k][...] if mode == "gather" else ins[k][:, me] if mode == "cross" else ins[k][me]
        outs[k][me] = kept
    if tail == "down":
        down(chans - 1).wait_recv()

        @pl.when(ending)
        def _():
            for c in range(chans - 1):
                down(c).start()

    if plug:
        plug.run()
    for k, (axes, mode) in enumerate(jobs):
        n, me = size_of(axes, sizes), index_of(axes, sizes)

        def finish(d, k=k, n=n, me=me):
            q = lax.rem(me + d, n)
            describe(k, q, q, q).wait()

        each(n, finish)
    if tail == "down":
        @pl.when(ending)
        def _():
            for c in range(chans):
                down(c).wait_send()
    if tail == "up":
        up(lax.axis_index("chan")).wait_send()

        @pl.when(ending)
        def _():
            for c in range(chans):
                up(c).wait_recv()


def signal_to(barrier, where):
    pl.semaphore_signal(barrier, inc=1, device_id=where, device_id_type=MESH)


def greet_line(barrier, n):
    me = lax.axis_index("seq")
    signal_to(barrier, {"seq": lax.rem(me + 1, n)})
    signal_to(barrier, {"seq": lax.rem(me + n - 1, n)})
    return 2


class Chain:
    counts = (3, 2, 6)
    pieces = 5

    def shapes(self, sizes, arrays):
        shape = jax.ShapeDtypeStruct(arrays[0].shape, BF)
        sems = [pltpu.SemaphoreType.DMA((self.pieces,)) for unused in range(4)]
        return [shape, shape], [pltpu.VMEM(shape.shape, BF)] * 2 + sems

    def bind(self, sizes, ins, outs, scratch):
        bound = Chain()
        bound.n, bound.ins, bound.outs, bound.scratch = sizes["seq"], ins, outs, scratch
        return bound

    def greet(self, barrier):
        return greet_line(barrier, self.n)

    def copy(self, way, piece):
        me = lax.axis_index("seq")
        rows = self.outs[0].shape[0] // self.pieces
        part = pl.ds(pl.multiple_of(piece * rows, rows), rows)
        target = lax.rem(me + 1, self.n) if way == 0 else lax.rem(me + self.n - 1, self.n)
        return pltpu.make_async_remote_copy(
            src_ref=self.scratch[way].at[part],
            dst_ref=self.outs[way].at[part],
            send_sem=self.scratch[2 + way].at[piece],
            recv_sem=self.scratch[4 + way].at[piece],
            device_id={"seq": target},
            device_id_type=MESH,
        )

    def start(self):
        me = lax.axis_index("seq")
        for way, edge in ((0, 0), (1, self.n - 1)):

            @pl.when(me == edge)
            def _(way=way):
                self.outs[way][...] = jnp.zeros(self.outs[way].shape, BF)

    def run(self):
        me = lax.axis_index("seq")
        rows = self.outs[0].shape[0] // self.pieces

        def beat(t):
            for way in (0, 1):
                place = me if way == 0 else self.n - 1 - me
                piece = t - place
                active = (piece >= 0) & (piece < self.pieces)

                @pl.when(active & (place > 0))
                def _(way=way, piece=piece):
                    self.copy(way, piece).wait_recv()

                @pl.when(active & (place < self.n - 1))
                def _(way=way, piece=piece):
                    part = pl.ds(pl.multiple_of(piece * rows, rows), rows)
                    before = self.outs[way][part, :].astype(F32)
                    term = self.ins[way][part, :].astype(F32)
                    self.scratch[way][part, :] = (self.ins[2][part, :] * before + term).astype(BF)
                    self.copy(way, piece).start()

        beat(0)
        each(self.n - 1 + self.pieces, beat)

        for way in (0, 1):

            @pl.when(me != (self.n - 1 if way == 0 else 0))
            def _(way=way):
                for piece in range(self.pieces):
                    self.copy(way, piece).wait_send()


class Grid:
    counts = (1, 1, 10)

    def shapes(self, sizes, arrays):
        d, n = sizes["dp"], sizes["seq"]
        shape = jax.ShapeDtypeStruct((d, n) + arrays[0].shape, BF)
        lengths = (n, d * n, d, d * n, n, n, d * n, d, d * n, d * n)
        return [shape], [pltpu.SemaphoreType.DMA((k,)) for k in lengths]

    def bind(self, sizes, ins, outs, scratch):
        bound = Grid()
        bound.d, bound.n = sizes["dp"], sizes["seq"]
        bound.src, bound.out, bound.sems = ins[0], outs[0], scratch
        return bound

    def greet(self, barrier):
        mine = lax.axis_index("dp")
        for e in range(1, self.d):
            signal_to(barrier, {"dp": lax.rem(mine + e, self.d)})
        return greet_line(barrier, self.n) + self.d - 1

    def copy(self, half, way, e, k, own=False, target=None):
        rows = self.src.shape[0]
        cut = (rows * 5 // 6) // 16 * 16
        part = pl.ds(0, cut) if half == 0 else pl.ds(cut, rows - cut)
        me = lax.axis_index("seq")
        slot = e * self.n + k
        if way == "cross":
            where = {"dp": lax.axis_index("dp") if target is None else target}
            recv = self.sems[1].at[slot] if half == 0 else self.sems[2].at[e]
            to = 0 if target is None else target
            send = self.sems[6].at[to * self.n + k] if half == 0 else self.sems[7].at[to]
        else:
            shift = 1 if way == "up" else self.n - 1
            where = {"seq": lax.rem(me + shift, self.n)}
            recv = self.sems[0].at[k] if half == 0 else self.sems[3].at[slot]
            ups = 4 if way == "up" else 5
            send = self.sems[ups].at[k] if half == 0 else self.sems[ups + 4].at[slot]
        src = self.src.at[part] if own else self.out.at[e, k, part]
        return pltpu.make_async_remote_copy(
            src_ref=src,
            dst_ref=self.out.at[e, k, part],
            send_sem=send,
            recv_sem=recv,
            device_id=where,
            device_id_type=MESH,
        )

    def partners(self):
        mine = lax.axis_index("dp")
        return [lax.rem(mine + e, self.d) for e in range(1, self.d)]

    def both(self, half, e, k, own=False):
        me = lax.axis_index("seq")

        @pl.when(me < self.n - 1)
        def _():
            self.copy(half, "up", e, k, own).start()

        @pl.when(me > 0)
        def _():
            self.copy(half, "down", e, k, own).start()

    def start(self):
        mine, me = lax.axis_index("dp"), lax.axis_index("seq")
        for e in self.partners():
            self.copy(1, "cross", mine, me, True, e).start()
        self.both(1, mine, me, True)
        self.both(0, mine, me, True)
        for e in self.partners():
            self.copy(0, "cross", mine, me, True, e).start()
        self.out[mine, me] = self.src[...]

    def run(self):
        mine, me, n = lax.axis_index("dp"), lax.axis_index("seq"), self.n
        others = self.partners()
        for e in others:
            self.copy(1, "cross", e, me, target=e).wait_recv()
            self.both(1, e, me)

        def hop(d):
            for way, k, there, onward in (
                ("up", me - d, me >= d, me < n - 1),
                ("down", me + d, me + d < n, me > 0),
            ):
                for e in [mine] + others:

                    @pl.when(there)
                    def _(way=way, k=k, e=e):
                        self.copy(1, way, e, k).wait_recv()

                    @pl.when(there & onward)
                    def _(way=way, k=k, e=e):
                        self.copy(1, way, e, k).start()

                @pl.when(there)
                def _(way=way, k=k):
                    self.copy(0, way, mine, k).wait_recv()

                @pl.when(there & onward)
                def _(way=way, k=k):
                    self.copy(0, way, mine, k).start()

                @pl.when(there)
                def _(way=way, k=k):
                    for e in others:
                        self.copy(0, "cross", mine, k, target=e).start()

        each(n, hop)

        def settle(k):
            for e in others:
                self.copy(0, "cross", e, k, target=e).wait_recv()
                self.copy(0, "cross", mine, k, target=e).wait_send()
            for way, sent in (("up", (k <= me) & (me < n - 1)), ("down", (k >= me) & (me > 0))):

                @pl.when(sent)
                def _(way=way, k=k):
                    self.copy(0, way, mine, k).wait_send()
                    for e in [mine] + others:
                        self.copy(1, way, e, k).wait_send()

        settle(0)
        each(n, settle)
        for e in others:
            self.copy(1, "cross", mine, me, target=e).wait_send()


def exchange(sizes, call_id, jobs, arrays, tail=None, tail_array=None, plug=None, plug_arrays=()):
    plan, out_shapes, sems = [], [], []
    for (axes, mode), array in zip(jobs, arrays):
        n = size_of(axes, sizes)
        shape = (n,) + array.shape if mode == "gather" else array.shape
        if mode == "cross":
            shape = (n, array.shape[0]) + array.shape[2:]
        plan.append((axes, mode))
        out_shapes.append(jax.ShapeDtypeStruct(shape, array.dtype))
        sems += [pltpu.SemaphoreType.DMA((n,)), pltpu.SemaphoreType.DMA((n,))]
    arrays = list(arrays)
    if tail:
        if tail == "up":
            arrays.append(tail_array)
            shape = (sizes["chan"],) + tail_array.shape
        else:
            shape = (PAD,) + arrays[0].shape[1:]
        out_shapes.append(jax.ShapeDtypeStruct(shape, arrays[0].dtype))
        sems += [pltpu.SemaphoreType.DMA((sizes["chan"],)), pltpu.SemaphoreType.DMA((sizes["chan"],))]
    if plug:
        arrays += plug_arrays
        plug_shapes, plug_scratch = plug.shapes(sizes, plug_arrays)
        out_shapes += plug_shapes
        sems += plug_scratch
    vmem = pl.BlockSpec(memory_space=pltpu.VMEM)
    return pl.pallas_call(
        functools.partial(exchange_kernel, tuple(plan), tail, plug, sizes),
        out_shape=out_shapes,
        in_specs=[vmem] * len(arrays),
        out_specs=[vmem] * len(out_shapes),
        scratch_shapes=sems,
        compiler_params=pltpu.CompilerParams(
            collective_id=call_id, has_side_effects=True, vmem_limit_bytes=LIMIT
        ),
        name=f"exchange_{call_id}",
    )(*arrays)


def mm(a, b, da, db):
    return lax.dot_general(
        a.astype(BF), b.astype(BF), (((da,), (db,)), ((), ())), preferred_element_type=F32
    )


def exact(a, b, da=1, db=0):
    return lax.dot_general(
        a, b, (((da,), (db,)), ((), ())), precision=HIGH, preferred_element_type=F32
    )


def softplus(v):
    return jnp.maximum(v, 0.0) + jnp.log1p(jnp.exp(-jnp.abs(v)))


def head_mask(width, heads_first):
    shape = (LANES, width) if heads_first else (width, LANES)
    head = lax.broadcasted_iota(jnp.int32, shape, 0 if heads_first else 1)
    column = lax.broadcasted_iota(jnp.int32, shape, 1 if heads_first else 0)
    return (column // HDIM == head).astype(F32)


def decays(raw, bias, decay_log):
    length = raw.shape[0]
    step = softplus(raw + bias)
    rate = jnp.exp(decay_log)
    row = lax.broadcasted_iota(jnp.int32, (length, length), 0)
    col = lax.broadcasted_iota(jnp.int32, (length, length), 1)
    lower = (row >= col).astype(F32)
    cumulative = exact(lower, -step * rate)
    return step, rate, cumulative, row, col, lower


def forward_kernel(
    inner_ref, mixer_ref, raw_ref, conv_inner_ref, conv_mixer_ref, bias_ref, log_ref, grad_ref,
    summed_inner_ref, summed_mixer_ref, state_ref, back_ref, decay_ref, wide_inner, wide_mixer,
):
    length = raw_ref.shape[0]
    width = conv_inner_ref.shape[1]
    taps = conv_inner_ref.shape[0]
    wide_inner[...] = inner_ref[...].astype(F32)
    wide_mixer[...] = mixer_ref[...].astype(F32)
    first = PAD - (taps - 1)

    def convolved(wide, kernel):
        total = kernel[0:1, :] * wide[pl.ds(first, length), :]
        for k in range(1, taps):
            total = total + kernel[k : k + 1, :] * wide[pl.ds(first + k, length), :]
        return total

    inner = convolved(wide_inner, conv_inner_ref)
    mixer = convolved(wide_mixer, conv_mixer_ref)
    summed_inner_ref[...] = inner
    summed_mixer_ref[...] = mixer
    act = inner * jax.nn.sigmoid(inner)
    mix = mixer * jax.nn.sigmoid(mixer)
    half = mix.shape[1] // 2
    step, rate, cumulative, row, col, lower = decays(raw_ref[...], bias_ref[...], log_ref[...])
    last = cumulative[length - 1 : length, :]
    spread = head_mask(width, True)
    tail = exact(jnp.exp(last - cumulative) * step, spread)
    grown = exact(jnp.exp(cumulative), spread)
    upstream = grad_ref[...].astype(F32)
    state_ref[...] = mm(act * tail, mix[:, :half], 0, 0).astype(BF)
    back_ref[...] = mm(grown * upstream, mix[:, half:], 0, 0).astype(BF)
    row_decay = jnp.sum(head_mask(width, False) * jnp.exp(last), axis=1, keepdims=True)
    decay_ref[...] = jnp.broadcast_to(row_decay, decay_ref.shape)


def backward_kernel(
    heads, inner_ref, mixer_ref, raw_ref, conv_inner_ref, conv_mixer_ref, bias_ref, log_ref,
    skip_ref, grad_ref, start_ref, end_ref,
    out_ref, step_ref, z_ref, y_ref, pad_inner, pad_mixer,
):
    length = raw_ref.shape[0]
    width = conv_inner_ref.shape[1]
    taps = conv_inner_ref.shape[0]
    spread = head_mask(width, True)
    spread_down = head_mask(width, False)
    start, end = start_ref[...].astype(F32), end_ref[...].astype(F32)
    inner, mixer = inner_ref[...], mixer_ref[...]
    inner_gate, mixer_gate = jax.nn.sigmoid(inner), jax.nn.sigmoid(mixer)
    act, mix = inner * inner_gate, mixer * mixer_gate
    half = mix.shape[1] // 2
    into, out_of = mix[:, :half], mix[:, half:]
    raw = raw_ref[...]
    step, rate, cumulative, row, col, lower = decays(raw, bias_ref[...], log_ref[...])
    last = cumulative[length - 1 : length, :]
    step_wide = exact(step, spread)
    grown = exact(jnp.exp(cumulative), spread)
    fading = exact(jnp.exp(last - cumulative), spread)
    upstream_low = grad_ref[...]
    upstream = upstream_low.astype(F32)
    stepped_low = (act * step_wide).astype(BF)
    stepped = stepped_low.astype(F32)
    scores = mm(out_of, into, 1, 1)
    causal = row >= col
    across = cumulative.T
    score_grad = jnp.zeros((length, length), F32)
    for h in range(heads):
        cols = slice(h * HDIM, (h + 1) * HDIM)
        gap = cumulative[:, h : h + 1] - across[h : h + 1, :]
        decay = jnp.where(causal, jnp.exp(jnp.where(causal, gap, 0.0)), 0.0)
        weights = (decay * scores).astype(BF)
        grad_h, step_h = upstream_low[:, cols], stepped_low[:, cols]
        score_grad = score_grad + decay * mm(grad_h, step_h, 1, 1)
        z_ref[:, cols] = mm(weights, grad_h, 0, 0)
        y_ref[:, cols] = mm(weights, step_h, 1, 0)
    z = z_ref[...]
    carried = grown * mm(out_of, start, 1, 1)
    ending = fading * mm(into, end, 1, 1)
    act_grad = step_wide * (z + ending) + exact(skip_ref[...], spread)[0:1, :] * upstream
    to_heads = functools.partial(exact, b=spread, da=1, db=1)
    step_grad = to_heads(act * (z + ending))
    tail_term = to_heads(stepped * ending)
    sum_grad = to_heads(upstream * (y_ref[...] + carried) - stepped * z) - tail_term
    held = jnp.sum(start * end, axis=1, keepdims=True)
    overall = jnp.sum(tail_term, axis=0, keepdims=True) + jnp.exp(last) * jnp.sum(
        spread_down * held, axis=0, keepdims=True
    )
    decay_grad = exact(lower, sum_grad, 0, 0) + overall
    step_grad = (step_grad - rate * decay_grad) * jax.nn.sigmoid(raw + bias_ref[...])
    out_grad = mm(score_grad, into, 1, 0) + mm(grown * upstream, start, 1, 0)
    into_grad = mm(score_grad, out_of, 0, 0) + mm(fading * stepped, end, 1, 0)
    inner_slope = inner_gate * (1.0 + inner * (1.0 - inner_gate))
    mixer_slope = mixer_gate * (1.0 + mixer * (1.0 - mixer_gate))
    for pad in (pad_inner, pad_mixer):
        pad[0:PAD, :] = jnp.zeros((PAD, pad.shape[1]), F32)
        pad[PAD + length :, :] = jnp.zeros((PAD, pad.shape[1]), F32)
    pad_inner[PAD : PAD + length, :] = act_grad * inner_slope
    pad_mixer[PAD : PAD + length, :half] = into_grad * mixer_slope[:, :half]
    pad_mixer[PAD : PAD + length, half:] = out_grad * mixer_slope[:, half:]

    def spread_back(pad, kernel):
        total = None
        for k in range(taps):
            term = kernel[k : k + 1, :] * pad[pl.ds(taps - 1 - k, PAD + length), :]
            total = term if total is None else total + term
        return total.astype(BF)

    mixer_end = width + 2 * half
    inner_back = spread_back(pad_inner, conv_inner_ref)
    out_ref[:, 0:width] = inner_back
    out_ref[0:PAD, 0:LANES] = (inner_back[0:PAD, 0:LANES].astype(F32) + step_grad.T[0:PAD, :]).astype(BF)
    out_ref[:, width:mixer_end] = spread_back(pad_mixer, conv_mixer_ref)
    step_ref[...] = step_grad.astype(BF)


def local_call(kernel, out_shapes, scratch, name, *arrays):
    vmem = pl.BlockSpec(memory_space=pltpu.VMEM)
    return pl.pallas_call(
        kernel,
        out_shape=out_shapes,
        in_specs=[vmem] * len(arrays),
        out_specs=jax.tree.map(lambda unused: vmem, out_shapes),
        scratch_shapes=scratch,
        compiler_params=pltpu.CompilerParams(vmem_limit_bytes=LIMIT),
        name=name,
    )(*arrays)


def rows_dot(gradient, weight):
    return lax.dot_general(
        gradient, weight, (((1,), (1,)), ((), ())), preferred_element_type=F32
    )


def body(
    sizes,
    layer_input,
    inner_weight,
    mixer_weight,
    step_weight,
    conv_inner,
    conv_mixer,
    step_bias,
    decay_log,
    skip_gain,
    output_grad,
):
    own = layer_input[0]
    rows, model = own.shape
    chans, seqs, dps = sizes["chan"], sizes["seq"], sizes["dp"]
    groups = dps * seqs
    length = rows * chans
    width = inner_weight.shape[1]
    mixed = mixer_weight.shape[1]
    heads = step_bias.shape[0]
    blocks = own.reshape(rows, dps, seqs, model // groups).transpose(1, 2, 0, 3)
    gathered, own_columns, history = exchange(
        sizes, 0, ((("chan",), "gather"), (("dp",), "swap")), (own, blocks), "down"
    )
    history = jnp.where(lax.axis_index("seq") > 0, history, jnp.zeros_like(history))
    tokens = jnp.concatenate([history, gathered.reshape(length, model)], axis=0)
    lane_pad = ((0, 0), (0, LANES - heads))
    step_wide = jnp.pad(step_weight, lane_pad)
    inner_proj = jnp.dot(tokens, inner_weight, preferred_element_type=F32).astype(BF)
    mixer_proj = jnp.dot(tokens, mixer_weight, preferred_element_type=F32).astype(BF)
    step_raw = jnp.dot(tokens[PAD:], step_wide, preferred_element_type=F32)
    vectors = jnp.pad(jnp.stack((step_bias, decay_log, skip_gain)), ((0, 5), lane_pad[1]))
    bias, rates, skips = vectors[0:1], vectors[1:2], vectors[2:3]
    upstream = output_grad[0]
    inner_sum, mixer_sum, state, back_state, decay = local_call(
        forward_kernel,
        (
            jax.ShapeDtypeStruct((length, width), F32),
            jax.ShapeDtypeStruct((length, mixed), F32),
            jax.ShapeDtypeStruct((width, mixed // 2), BF),
            jax.ShapeDtypeStruct((width, mixed // 2), BF),
            jax.ShapeDtypeStruct((width, mixed // 2), F32),
        ),
        [pltpu.VMEM((PAD + length, width), F32), pltpu.VMEM((PAD + length, mixed), F32)],
        "forward",
        inner_proj, mixer_proj, step_raw, conv_inner, conv_mixer, bias, rates, upstream,
    )
    columns, start, end = exchange(
        sizes,
        1,
        ((("seq",), "cross"),),
        (own_columns,),
        plug=Chain(),
        plug_arrays=(state, back_state, decay),
    )
    assert length == LANES and heads + conv_inner.shape[0] - 1 <= PAD
    grads, step_grads = local_call(
        functools.partial(backward_kernel, heads),
        (
            jax.ShapeDtypeStruct((PAD + length, width + mixed), BF),
            jax.ShapeDtypeStruct((length, LANES), BF),
        ),
        [
            pltpu.VMEM((length, width), F32),
            pltpu.VMEM((length, width), F32),
            pltpu.VMEM((2 * PAD + length, width), F32),
            pltpu.VMEM((2 * PAD + length, mixed), F32),
        ],
        "backward",
        inner_sum, mixer_sum, step_raw, conv_inner, conv_mixer, bias, rates,
        jnp.broadcast_to(skips, (8, LANES)), upstream, start, end,
    )
    partial = rows_dot(grads[:, :width], inner_weight)
    partial = partial + rows_dot(grads[:, width:], mixer_weight)
    main_part = (partial[PAD:] + rows_dot(step_grads, step_wide)).astype(BF)
    tail_part = partial[:PAD].astype(BF)
    parts = main_part.reshape(chans, rows, model)
    parts, columns, tails, all_grads = exchange(
        sizes,
        2,
        ((("chan",), "swap"), (("chan",), "gather")),
        (parts, columns),
        "up",
        tail_part,
        Grid(),
        (grads,),
    )
    total = jnp.sum(parts.astype(F32), axis=0)
    reached = (lax.axis_index("chan") == chans - 1) & (lax.axis_index("seq") < seqs - 1)
    live = lax.broadcasted_iota(jnp.int32, (PAD, 1), 0) > PAD - conv_inner.shape[0]
    tail_sum = jnp.where(reached & live, jnp.sum(tails.astype(F32), axis=0), 0.0)
    total = jnp.concatenate([total[: rows - PAD], total[rows - PAD :] + tail_sum], axis=0)
    input_grad = total.astype(BF)

    split = all_grads
    main, early = split[:, :, PAD:], jnp.where(live, split[:, :, :PAD], 0)
    steps = split[:, :, :heads, :LANES].transpose(0, 1, 3, 2).reshape(groups * length, heads)
    early = jnp.concatenate([early[:, 1:], jnp.zeros_like(early[:, :1])], axis=1)
    final = (main[:, :, length - PAD :].astype(F32) + early.astype(F32)).astype(BF)
    main = jnp.concatenate([main[:, :, : length - PAD], final], axis=2)
    main = main.reshape(groups * length, -1)
    columns = columns.transpose(2, 1, 0, 3, 4).reshape(groups * length, model // groups)
    norm_factor = 1.0 / math.sqrt(groups * length)

    def term(right):
        dims = (((0,), (0,)), ((), ()))
        return norm_factor * lax.dot_general(columns, right, dims, preferred_element_type=F32)

    mixer_terms = term(main[:, width:]).reshape(chans, -1, mixed)
    (mixer_parts,) = exchange(sizes, 3, ((("chan",), "swap"),), (mixer_terms,))
    mixer_weight_grad = jnp.sum(mixer_parts, axis=0)
    return (
        input_grad[None],
        term(main[:, :width]),
        mixer_weight_grad,
        term(steps),
    )


def solution(mesh):
    sizes = dict(mesh.shape)
    in_specs = (
        P("dp", ("seq", "chan"), None),
        P(None, "chan"),
        P(),
        P(None, "chan"),
        P(None, "chan"),
        P(),
        P("chan"),
        P("chan"),
        P("chan"),
        P("dp", "seq", "chan"),
    )
    out_specs = (
        P("dp", ("seq", "chan"), None),
        P(("dp", "seq"), "chan"),
        P(("dp", "seq", "chan"), None),
        P(("dp", "seq"), "chan"),
    )
    return jax.shard_map(
        functools.partial(body, sizes),
        mesh=mesh,
        in_specs=in_specs,
        out_specs=out_specs,
        check_vma=False,
    )
```

time: 440 us -> 126 us (0.29)
  waiting for transfers between devices: 281 us -> 0 us
  Pallas kernels: 0 us -> 94.5 us
  blocking collectives: 61.7 us -> 0 us
  starting transfers between devices: 20.2 us -> 0 us
  between operations: 16 us -> 0.82 us
  matrix products: 29.3 us -> 14.4 us
  local copies, waits for them, and re-layouts: 20.6 us -> 7.62 us
    unnamed x8 -> x0, waiting for transfers between devices: 237 us -> none
    pallas_call x0 -> x6, Pallas kernels: none -> 94.5 us  [the longest x4 85.9 us: exchange(): pl.pallas_call(functools.partial(exchange_kernel, tuple(plan), tail, plug...]
    all_gather x5 -> x0, blocking collectives: 54.3 us -> none  [the longest x2 25.9 us: prefix(): lax.all_gather(a.astype(kind), axis)]
    all_gather x2 -> x0, waiting for transfers between devices: 25.4 us -> none  [the longest x1 19.5 us: body(): lax.all_gather(inner_weight, 'chan', axis=1, tiled=True)]
    unnamed x91 -> x14, local copies, waits for them, and re-layouts: 18.1 us -> 0.91 us
    dot_general x22 -> x9, matrix products: 29.3 us -> 14.4 us  [the longest x3 4.85 us: rows_dot(): lax.dot_general(gradient, weight, (((1,), (1,)), ((), ())), preferred_ele...]
    all_to_all x3 -> x0, waiting for transfers between devices: 10.3 us -> none  [the longest x1 7.04 us: body(): lax.all_to_all(grad_inner, 'chan', split_axis=0, concat_axis=1, tiled=True)]
    ppermute x4 -> x0, starting transfers between devices: 9.96 us -> none  [from_behind(): lax.ppermute(value, axis, [(source, source + steps) for source in range(f...]
  transfers between devices with their start and end apart: 12 -> 0, of which waited for: 8 -> 0; matrix products, arithmetic and copies ran while one was open for 10% -> 0% of each run, Pallas kernels for 0% -> 0%
where the time goes in v1:
time: 126 us; the launch traced here: 125 us
  Pallas kernels  94.5 us (75%)
  matrix products  14.4 us (11%)
  local copies, waits for them, and re-layouts  7.62 us (6%)
  other arithmetic  7.56 us (6%)
    pallas_call x4, Pallas kernels, exchange(): pl.pallas_call(functools.partial(exchange_kernel, tuple(plan), tail, plug...  85.9 us
    pallas_call x2, Pallas kernels, local_call(): pl.pallas_call(kernel, out_shape=out_shapes, in_specs=[vmem] * len(arrays...  8.6 us
    dot_general x3, matrix products, rows_dot(): lax.dot_general(gradient, weight, (((1,), (1,)), ((), ())), preferred_ele...  4.85 us
    dot_general x3, matrix products, term(): lax.dot_general(columns, right, dims, preferred_element_type=F32)  3.57 us
    dot_general x1, matrix products, body(): jnp.dot(tokens, mixer_weight, preferred_element_type=F32).astype(BF)  2.58 us

profile of v1, /device:TPU:0, one launch (start us, length us, event | category | flops | bytes accessed | tf_op | source)
XLA Modules:
  0.0 124.9 jit_solution(10790694993485800842)
XLA Ops:
  0.7 0.9 select_maximum_fusion
  2.7 1.1 reshape_squeeze.3
  4.6 16.7 %exchange_0.1 = (bf16[4,32,2560]{2,1,0:T(8,128)(2,1)}, bf16[2,4,32,320]{3,2,1,0:T(8,128)(2,1)}, bf16[16,2560]{1,0:T(8,128)(2,1)}) custom-call(bf16[32,2560]{1,0:T(8,128)(2,1)} %bitcast.44, bf16[2,4,32,320]{3,2,1,0:T(8,128)(2,1)} %bitcast.41), custom_call_target="tpu_custom_call" | custom-call | tf_op jit(solution)/shard_map/exchange_0/pallas_call | solution.py:420
  21.4 2.0 %fusion.7.raw_ref = f32[128,128]{1,0:T(8,128)} fusion(bf16[128,2560]{1,0:T(8,128)(2,1)} %bitcast.49, bf16[2560,10]{0,1:T(8,128)(2,1)} %param.13), kind=kOutput, calls=%fused_computation.13 | convolution fusion | flops 83886080 | bytes 772096 | tf_op jit(solution)/shard_map/dot_general | solution.py:632
  23.4 2.6 %convolution_convert_fusion.1.mixer_ref = bf16[144,256]{1,0:T(8,128)(2,1)} fusion(bf16[2560,256]{1,0:T(8,128)(2,1)} %param.12, bf16[128,2560]{1,0:T(8,128)(2,1)} %bitcast.50, bf16[16,2560]{1,0:T(8,128)(2,1)S(1)} %broadcast_select_fusion), kind=kOutput, calls=%fused_computation.10 | convolution fusion | flops 190255104 | bytes 2121728 | tf_op jit(solution)/shard_map/dot_general | solution.py:631
  26.0 1.4 %convolution_convert_fusion.inner_ref = bf16[144,640]{1,0:T(8,128)(2,1)} fusion(bf16[2560,640]{1,0:T(8,128)(2,1)S(1)} %copy-done, bf16[128,2560]{1,0:T(8,128)(2,1)S(1)} %bitcast.51, bf16[16,2560]{1,0:T(8,128)(2,1)S(1)} %broadcast_select_fusion), kind=kOutput, calls=%fused_computation.9 | convolution fusion | flops 473425920 | bytes 4198400 | tf_op jit(solution)/shard_map/dot_general | solution.py:630
  27.4 3.1 %forward.1 = (f32[128,640]{1,0:T(8,128)}, f32[128,256]{1,0:T(8,128)}, bf16[640,128]{1,0:T(8,128)(2,1)}, bf16[640,128]{1,0:T(8,128)(2,1)}, f32[640,128]{1,0:T(8,128)}) custom-call(bf16[144,640]{1,0:T(8,128)(2,1)} %convolution_convert_fusion.inner_ref, bf16[144,256]{1,0:T(8,128)(2,1)} %convolution_convert_fusion.1.mixer_ref, f32[128,128]{1,0:T(8,128)} %fusion.7.raw_ref, ...), custom_call_target="tpu_custom_call" | custom-call | tf_op jit(solution)/shard_map/forward/pallas_call | solution.py:584
  30.5 26.8 %exchange_1.1 = (bf16[4,2,32,320]{3,2,1,0:T(8,128)(2,1)}, bf16[640,128]{1,0:T(8,128)(2,1)}, bf16[640,128]{1,0:T(8,128)(2,1)}) custom-call(bf16[2,4,32,320]{3,2,1,0:T(8,128)(2,1)} %get-tuple-element.25.refs_0_, bf16[640,128]{1,0:T(8,128)(2,1)} %get-tuple-element.26.refs_1_, bf16[640,128]{1,0:T(8,128)(2,1)} %get-tuple-element.27.refs_2_, ...), custom_call_target="tpu_custom_call" | custom-call | tf_op jit(solution)/shard_map/exchange_1/pallas_call | solution.py:420
  57.2 5.5 %backward.1 = (bf16[144,896]{1,0:T(8,128)(2,1)}, bf16[128,128]{1,0:T(8,128)(2,1)}) custom-call(f32[128,640]{1,0:T(8,128)} %get-tuple-element.23.inner_ref, f32[128,256]{1,0:T(8,128)} %get-tuple-element.24.mixer_ref, f32[128,128]{1,0:T(8,128)} %fusion.7.raw_ref, f32[4,640]{1,0:T(4,128)} %conv_inner_ref.3, f32[4,256]{1,0:T(4,128)} %conv_mixer_ref.3, ...), custom_call_target="tpu_custom_call" | custom-call | tf_op jit(solution)/shard_map/backward/pallas_call | solution.py:584
  62.7 2.2 %fusion.10 = f32[144,2560]{1,0:T(8,128)S(1)} fusion(bf16[2560,640]{1,0:T(8,128)(2,1)S(1)} %copy-done, bf16[144,896]{1,0:T(8,128)(2,1)} %get-tuple-element.31.refs_3_), kind=kOutput, calls=%fused_computation.20 | convolution fusion | flops 471859200 | bytes 4935680 | tf_op jit(solution)/shard_map/dot_general | solution.py:596
  65.0 1.5 %convolution_add_fusion = f32[144,2560]{1,0:T(8,128)S(1)} fusion(f32[144,2560]{1,0:T(8,128)S(1)} %fusion.10, bf16[2560,256]{1,0:T(8,128)(2,1)S(1)} %copy-done.2, bf16[144,896]{1,0:T(8,128)(2,1)} %get-tuple-element.31.refs_3_), kind=kOutput, calls=%fused_computation | convolution fusion | flops 189112320 | bytes 4333568 | tf_op jit(solution)/shard_map/dot_general | solution.py:596
  67.2 1.1 fusion
  68.3 34.0 %exchange_2.1 = (bf16[4,32,2560]{2,1,0:T(8,128)(2,1)}, bf16[4,4,2,32,320]{4,3,2,1,0:T(8,128)(2,1)}, bf16[4,16,2560]{2,1,0:T(8,128)(2,1)}, bf16[2,4,144,896]{3,2,1,0:T(8,128)(2,1)}) custom-call(bf16[4,32,2560]{2,1,0:T(8,128)(2,1)} %bitcast.37, bf16[4,2,32,320]{3,2,1,0:T(8,128)(2,1)} %get-tuple-element.33.refs_1_, bf16[16,2560]{1,0:T(8,128)(2,1)} %slice.100.refs_2_, ...), custom_call_target="tpu_custom_call" | custom-call | tf_op jit(solution)/shard_map/exchange_2/pallas_call | solution.py:420
  102.3 1.9 %convert_reduce_fusion = f32[32,2560]{1,0:T(8,128)} fusion(bf16[4,32,2560]{2,1,0:T(8,128)(2,1)} %get-tuple-element.34), kind=kLoop, calls=%fused_computation.6 | loop fusion | flops 573440 | bytes 983040 | tf_op jit(solution)/shard_map/reduce_sum | solution.py:689
  105.0 1.1 fusion.13
  106.1 1.0 convert_reduce_fusion.1
  107.1 1.0 fusion.14
  108.8 1.0 slice.64
  110.4 0.9 copy-done.3
  111.3 0.8 convolution_multiply_fusion.1
  112.2 1.1 convolution_multiply_fusion
  113.3 1.6 %fusion.3 = f32[320,640]{1,0:T(8,128)} fusion(bf16[1024,320]{1,0:T(8,128)(2,1)S(1)} %bitcast.36, bf16[1024,896]{1,0:T(8,128)(2,1)S(1)} %bitcast.39), kind=kOutput, calls=%fused_computation.7 | convolution fusion | flops 419635200 | bytes 2916352 | tf_op jit(solution)/shard_map/dot_general | solution.py:708
  114.9 8.4 %exchange_3.1 = f32[4,80,256]{2,1,0:T(8,128)} custom-call(f32[4,80,256]{2,1,0:T(8,128)} %bitcast.45), custom_call_target="tpu_custom_call" | custom-call | tf_op jit(solution)/shard_map/exchange_3/pallas_call | solution.py:420
  123.3 1.6 %reduce_sum.29 = f32[80,256]{1,0:T(8,128)} reduce(f32[4,80,256]{2,1,0:T(8,128)} %exchange_3.1, f32[]{:T(128)} %constant.6.clone.1), dimensions={0}, to_apply=%region_2.3 | reduce | flops 61440 | bytes 409604 | tf_op jit(solution)/shard_map/reduce_sum | solution.py:712
  (29 shorter events, 4.7 us)
Async XLA Ops:
  0.6 25.3 %copy-start = (bf16[2560,640]{1,0:T(8,128)(2,1)S(1)}, bf16[2560,640]{1,0:T(8,128)(2,1)}, u32[]{:S(2)}) copy-start(bf16[2560,640]{1,0:T(8,128)(2,1)} %param.11) | copy-start | bytes 9830404
  23.4 2.6 %copy-start.6 = (bf16[4,32,2560]{2,1,0:T(8,128)(2,1)S(1)}, bf16[4,32,2560]{2,1,0:T(8,128)(2,1)}, u32[]{:S(2)}) copy-start(bf16[4,32,2560]{2,1,0:T(8,128)(2,1)} %get-tuple-element.22) | copy-start | bytes 1966084
  62.7 2.2 %copy-start.2 = (bf16[2560,256]{1,0:T(8,128)(2,1)S(1)}, bf16[2560,256]{1,0:T(8,128)(2,1)}, u32[]{:S(2)}) copy-start(bf16[2560,256]{1,0:T(8,128)(2,1)} %param.12) | copy-start | bytes 3932164
  65.0 2.2 %copy-start.4 = (bf16[2560,10]{0,1:T(8,128)(2,1)S(1)}, bf16[2560,10]{0,1:T(8,128)(2,1)}, u32[]{:S(2)}) copy-start(bf16[2560,10]{0,1:T(8,128)(2,1)} %param.13) | copy-start | bytes 153604
  65.0 2.2 %copy-start.5 = (bf16[128,128]{1,0:T(8,128)(2,1)S(1)}, bf16[128,128]{1,0:T(8,128)(2,1)}, u32[]{:S(2)}) copy-start(bf16[128,128]{1,0:T(8,128)(2,1)} %get-tuple-element.32) | copy-start | bytes 98308
  105.0 4.9 %copy-start.1 = (bf16[2,4,144,896]{3,2,1,0:T(8,128)(2,1)S(1)}, bf16[2,4,144,896]{3,2,1,0:T(8,128)(2,1)}, u32[]{:S(2)}) copy-start(bf16[2,4,144,896]{3,2,1,0:T(8,128)(2,1)} %get-tuple-element.37) | copy-start | bytes 6193156
  110.1 1.1 copy-start.3
